TPU v7x, 256 devices: a whole 4x4x8 slice. The times are simulated.
256 devices in a mesh: dp: 32 (over y, x, core), seq: 8 (over z).
Axes of the slice: x: 4, y: 4, z: 8, core: 2. Of those that a mesh axis runs over, the one named last changes fastest.
Arguments:
- query_rows: bfloat16 [32, 1024, 3072], P('dp', 'seq'), may hold values from -6 to 6
- key_rows: bfloat16 [32, 1024, 3072], P('dp', 'seq'), may hold values from -6 to 6
- value_rows: bfloat16 [32, 1024, 3072], P('dp', 'seq'), may hold values from -6 to 6
- out_grad: bfloat16 [32, 1024, 6144], P('dp', 'seq'), may hold values from -54 to 54
- clip_lengths: int32 [32, 4], P('dp'), may hold values from 1 to 512, 1024 in all within a row
- out_weight: bfloat16 [3072, 6144], P('seq'), may hold values from -0.109375 to 0.109375
- query_gain: float32 [128], replicated, may hold values from 0.1 to 1.9
- key_gain: float32 [128], replicated, may hold values from 0.1 to 1.9
Outputs:
- query_grad: bfloat16 [32, 1024, 3072], P('dp', 'seq')
- key_grad: bfloat16 [32, 1024, 3072], P('dp', 'seq')
- value_grad: bfloat16 [32, 1024, 3072], P('dp', 'seq')
- weight_grad: float32 [3072, 6144], P('seq', 'dp')
- querygain_grad: float32 [128], replicated
- keygain_grad: float32 [128], replicated
- grad_norm: float32 [], replicated
Inputs may be any that keep to these rules, and one draw needn't show every extreme that they name: `clip_lengths`: the token counts of each group's clips sum to 1024.
All inputs are finite; a program needn't handle non-finite values.
Results may differ from a plain program's by a relative error of at most 0.015.
Values may be sent and summed in bfloat16 or wider, within the bound.
A program may use at most 128 MiB of HBM per device.

v0:
```python
import jax
import jax.numpy as jnp
from jax import lax
from jax.sharding import Mesh
from jax.sharding import PartitionSpec as P

HEAD_DIM = 128
MAX_NORM = 768
DP = ("dp_0", "dp_1", "dp_2")
DP_SEQ = ("dp_0", "dp_1", "dp_2", "seq")
EPS = 1e-06


def one_axis_at_a_time(array, axes):
    for axis in axes:
        array = lax.psum(array, axis)
    return array


def segment_ids(lengths, total):
    ends = jnp.cumsum(lengths)
    places = jnp.arange(total, dtype=jnp.int32)
    return jnp.sum((places[:, None] >= ends[None, :]).astype(jnp.int32), axis=1)


def norm_rows(rows, gain):
    wide = rows.astype(jnp.float32)
    inverse = lax.rsqrt(jnp.mean(wide * wide, axis=-1, keepdims=True) + EPS)
    unit = wide * inverse
    return (unit, inverse, (unit * gain).astype(jnp.bfloat16))


def norm_back(unit, inverse, gain, d_norm):
    gain_part = jnp.sum(unit * d_norm, axis=(0, 1))
    d_unit = d_norm * gain
    d_rows = inverse * (d_unit - unit * jnp.mean(unit * d_unit, axis=-1, keepdims=True))
    return (d_rows.astype(jnp.bfloat16), gain_part)


def local(
    query_rows, key_rows, value_rows, out_grad, clip_lengths, out_weight, query_gain, key_gain
):
    query, keys, values = (
        lax.all_to_all(query_rows[0], "seq", split_axis=1, concat_axis=0, tiled=True),
        lax.all_to_all(key_rows[0], "seq", split_axis=1, concat_axis=0, tiled=True),
        lax.all_to_all(value_rows[0], "seq", split_axis=1, concat_axis=0, tiled=True),
    )
    total = query.shape[0]
    heads = query.shape[1] // HEAD_DIM
    width = heads * HEAD_DIM
    scale = HEAD_DIM ** (-0.5)
    block = min(512, total)
    blocks = total // block
    seg = segment_ids(clip_lengths[0], total)
    q_unit, q_inv, q_norm = norm_rows(query.reshape(total, heads, HEAD_DIM), query_gain)
    k_unit, k_inv, k_norm = norm_rows(keys.reshape(total, heads, HEAD_DIM), key_gain)
    values3 = values.reshape(total, heads, HEAD_DIM)

    def forward_block(index):
        start = index * block
        query_block = lax.dynamic_slice_in_dim(q_norm, start, block, 0)
        seg_block = lax.dynamic_slice_in_dim(seg, start, block, 0)
        scores = (
            jnp.einsum("qhd,khd->hqk", query_block, k_norm, preferred_element_type=jnp.float32)
            * scale
        )
        same = seg_block[:, None] == seg[None, :]
        expo = jnp.where(same[None], jnp.exp(scores), 0.0)
        probs = (expo / jnp.sum(expo, axis=-1, keepdims=True)).astype(jnp.bfloat16)
        attn_out = jnp.einsum("hqk,khd->qhd", probs, values3, preferred_element_type=jnp.float32)
        return (probs, attn_out.astype(jnp.bfloat16))

    probs_all, attn_blocks = lax.map(forward_block, jnp.arange(blocks, dtype=jnp.int32))
    attn_flat = attn_blocks.reshape(total, width)
    out_full = lax.all_gather(out_grad[0], "seq", axis=0, tiled=True)
    weight_part = jnp.dot(attn_flat.T, out_full, preferred_element_type=jnp.float32)
    d_attn = jnp.dot(out_full, out_weight.T, preferred_element_type=jnp.float32).astype(
        jnp.bfloat16
    )
    d_attn3 = d_attn.reshape(total, heads, HEAD_DIM)

    def backward_block(carry, items):
        d_key, d_value = carry
        probs, index = items
        start = index * block
        attn_grad = lax.dynamic_slice_in_dim(d_attn3, start, block, 0)
        query_block = lax.dynamic_slice_in_dim(q_norm, start, block, 0)
        d_probs = jnp.einsum("qhd,khd->hqk", attn_grad, values3, preferred_element_type=jnp.float32)
        probs32 = probs.astype(jnp.float32)
        row_sum = jnp.sum(probs32 * d_probs, axis=-1, keepdims=True)
        d_scores = (probs32 * (d_probs - row_sum) * scale).astype(jnp.bfloat16)
        d_value = d_value + jnp.einsum(
            "hqk,qhd->khd", probs, attn_grad, preferred_element_type=jnp.float32
        )
        d_key = d_key + jnp.einsum(
            "hqk,qhd->khd", d_scores, query_block, preferred_element_type=jnp.float32
        )
        d_query = jnp.einsum("hqk,khd->qhd", d_scores, k_norm, preferred_element_type=jnp.float32)
        return ((d_key, d_value), d_query)

    empty = jnp.zeros((total, heads, HEAD_DIM), jnp.float32)
    (d_knorm, d_value32), d_query_blocks = lax.scan(
        backward_block, (empty, empty), (probs_all, jnp.arange(blocks, dtype=jnp.int32))
    )
    d_qnorm = d_query_blocks.reshape(total, heads, HEAD_DIM)
    query_grad, q_gain_part = norm_back(q_unit, q_inv, query_gain, d_qnorm)
    key_grad, k_gain_part = norm_back(k_unit, k_inv, key_gain, d_knorm)
    value_grad = d_value32.astype(jnp.bfloat16)
    query_back, key_back, value_back = (
        lax.all_to_all(
            query_grad.reshape(total, width), "seq", split_axis=0, concat_axis=1, tiled=True
        ),
        lax.all_to_all(
            key_grad.reshape(total, width), "seq", split_axis=0, concat_axis=1, tiled=True
        ),
        lax.all_to_all(
            value_grad.reshape(total, width), "seq", split_axis=0, concat_axis=1, tiled=True
        ),
    )
    weight_shard = lax.psum_scatter(
        weight_part.astype(jnp.bfloat16), DP, scatter_dimension=1, tiled=True
    ).astype(jnp.float32)
    local_squares = jnp.sum(weight_shard * weight_shard)
    qgain_raw, kgain_raw = (
        one_axis_at_a_time(q_gain_part, DP_SEQ),
        one_axis_at_a_time(k_gain_part, DP_SEQ),
    )
    weight_squares = one_axis_at_a_time(local_squares, DP_SEQ)
    squares = weight_squares + jnp.sum(qgain_raw * qgain_raw) + jnp.sum(kgain_raw * kgain_raw)
    grad_norm = jnp.sqrt(squares)
    factor = jnp.minimum(jnp.float32(1.0), MAX_NORM / (grad_norm + EPS))
    return (
        query_back[None],
        key_back[None],
        value_back[None],
        weight_shard * factor,
        qgain_raw * factor,
        kgain_raw * factor,
        grad_norm,
    )


def solution(mesh):
    torus = Mesh(mesh.devices.reshape(4, 4, 2, mesh.shape["seq"]), ("dp_0", "dp_1", "dp_2", "seq"))
    return jax.shard_map(
        local,
        mesh=torus,
        in_specs=(
            P(DP, "seq", None),
            P(DP, "seq", None),
            P(DP, "seq", None),
            P(DP, "seq", None),
            P(DP, None),
            P("seq", None),
            P(),
            P(),
        ),
        out_specs=(
            P(DP, "seq", None),
            P(DP, "seq", None),
            P(DP, "seq", None),
            P("seq", DP),
            P(),
            P(),
            P(),
        ),
        check_vma=False,
    )
```

profile of v0, /device:TPU:32, one launch (start us, length us, event | category | flops | bytes accessed | tf_op | source)
XLA Modules:
  0.0 430.5 jit_solution(6281215837916845542)
XLA Ops:
  9.5 8.6 %all-to-all-start = ((bf16[128,8,384]{0,2,1:T(8,128)(2,1)}), bf16[128,8,384]{0,2,1:T(8,128)(2,1)S(1)}, u32[]{:S(2)}, u32[]{:S(2)}) async-start(bf16[128,8,384]{0,2,1:T(8,128)(2,1)} %bitcast.4), calls=%async_computation | async-start | bytes 1572864 | tf_op jit(solution)/shard_map/all_to_all | solution.py:44
  19.2 26.2 %all-to-all-done = bf16[128,8,384]{0,2,1:T(8,128)(2,1)S(1)} async-done(((bf16[128,8,384]{0,2,1:T(8,128)(2,1)}), bf16[128,8,384]{0,2,1:T(8,128)(2,1)S(1)}, u32[]{:S(2)}, u32[]{:S(2)}) %all-to-all-start) | async-done | bytes 786464 | tf_op jit(solution)/shard_map/all_to_all | solution.py:44
  45.4 5.8 %all-to-all-start.1 = ((bf16[128,8,384]{0,2,1:T(8,128)(2,1)}), bf16[128,8,384]{0,2,1:T(8,128)(2,1)S(1)}, u32[]{:S(2)}, u32[]{:S(2)}) async-start(bf16[128,8,384]{0,2,1:T(8,128)(2,1)} %bitcast.8), calls=%async_computation.1 | async-start | bytes 1572864 | tf_op jit(solution)/shard_map/all_to_all | solution.py:45
  52.3 30.0 %all-to-all-done.1 = bf16[128,8,384]{0,2,1:T(8,128)(2,1)S(1)} async-done(((bf16[128,8,384]{0,2,1:T(8,128)(2,1)}), bf16[128,8,384]{0,2,1:T(8,128)(2,1)S(1)}, u32[]{:S(2)}, u32[]{:S(2)}) %all-to-all-start.1) | async-done | bytes 786464 | tf_op jit(solution)/shard_map/all_to_all | solution.py:45
  82.4 5.3 %all-to-all-start.2 = ((bf16[128,8,384]{0,2,1:T(8,128)(2,1)}), bf16[128,8,384]{0,2,1:T(8,128)(2,1)}, u32[]{:S(2)}, u32[]{:S(2)}) async-start(bf16[128,8,384]{0,2,1:T(8,128)(2,1)} %bitcast.10), calls=%async_computation.2 | async-start | bytes 1572864 | tf_op jit(solution)/shard_map/all_to_all | solution.py:46
  89.1 1.6 reshape.182
  90.7 1.2 convert_bitcast_fusion
  92.0 2.1 copy.147
  94.1 1.5 reshape.183
  97.4 2.3 copy.151
  99.7 19.1 %all-to-all-done.2 = bf16[128,8,384]{0,2,1:T(8,128)(2,1)} async-done(((bf16[128,8,384]{0,2,1:T(8,128)(2,1)}), bf16[128,8,384]{0,2,1:T(8,128)(2,1)}, u32[]{:S(2)}, u32[]{:S(2)}) %all-to-all-start.2) | async-done | bytes 786464 | tf_op jit(solution)/shard_map/all_to_all | solution.py:46
  118.7 2.5 copy.149
  121.2 2.2 reshape.177
  123.4 2.3 copy.152
  125.7 1.7 multiply_reduce_fusion.5
  128.8 21.1 %while.27 = (s32[]{:T(128)}, bf16[2,3,512,1024]{3,2,1,0:T(8,128)(2,1)}, bf16[2,512,3,128]{3,1,2,0:T(8,128)(2,1)}, s32[2]{0:T(128)S(1)}, s32[1024]{0:T(1024)S(1)}...) while((s32[]{:T(128)}, ...), condition=%wide.region_6.7_spmd, body=%wide.region_4.6_spmd.sunk | while | flops 817035776 | bytes 85746000 | solution.py:73
  130.5 3.4 fusion.75
  134.0 1.9 bitcast_dynamic-update-slice_fusion.2
  137.0 1.5 copy-done.1
  141.1 3.4 fusion.75
  144.5 1.9 bitcast_dynamic-update-slice_fusion.2
  147.6 1.5 copy-done.1
  149.9 3.1 copy.167
  153.0 2.1 copy.180
  155.3 1.5 copy.176
  156.8 32.1 %all-gather.3.cloned.1.call-done = bf16[1,1024,6144]{2,1,0:T(8,128)(2,1)} async-done(((bf16[1,128,6144]{2,1,0:T(8,128)(2,1)}), bf16[1,1024,6144]{2,1,0:T(8,128)(2,1)}) %all-gather.3.cloned.1.call-update) | async-done | bytes 12582928 | tf_op jit(solution)/shard_map/all_gather | solution.py:75
  188.9 11.4 %fusion.42 = bf16[384,6144]{0,1:T(8,128)(2,1)} fusion(bf16[1024,384]{0,1:T(8,128)(2,1)} %bitcast.161, bf16[1,1024,6144]{2,1,0:T(8,128)(2,1)} %all-gather.3.cloned.1.call-done), kind=kOutput, calls=%fused_computation.45 | convolution fusion | flops 4834197504 | bytes 18087936 | tf_op jit(solution)/shard_map/dot_general | solution.py:76
  200.3 10.4 %fusion.48 = bf16[1024,384]{0,1:T(8,128)(2,1)} fusion(bf16[384,6144]{1,0:T(8,128)(2,1)} %param.17, bf16[1,1024,6144]{2,1,0:T(8,128)(2,1)} %all-gather.3.cloned.1.call-done), kind=kOutput, calls=%fused_computation.62 | convolution fusion | flops 4832231424 | bytes 18087936 | tf_op jit(solution)/shard_map/dot_general | solution.py:77
  210.8 57.7 %while.28 = (s32[]{:T(128)}, f32[1024,3,128]{0,2,1:T(8,128)}, f32[1024,3,128]{0,2,1:T(8,128)S(1)}, f32[2,512,3,128]{3,1,2,0:T(8,128)}, s32[2]{0:T(128)S(1)}, /*i...) while((s32[]{:T(128)}, f32[1024,3,128]{0,2,1:T(8,128)}, ...), condition=%wide.region_9.10_spmd.clone, body=%wide.region_7.9_spmd.clone.sunk | while | flops 1634210816 | bytes 57019604 | solution.py:102
  212.0 5.0 %fusion.83 = f32[3,512,1024]{2,1,0:T(8,128)} fusion(bf16[1024,3,128]{2,0,1:T(8,128)(2,1)} %get-tuple-element.549, bf16[1024,3,128]{0,2,1:T(8,128)(2,1)} %get-tuple-element.548, s32[]{:T(128)S(6)} %select_n.24), kind=kOutput, calls=%fused_computation.30.clone.1 | convolution fusion | flops 402653184 | bytes 7471108 | tf_op jit(solution)/shard_map/while/body/eval_jaxpr/qhd,khd->hqk/dot_general | solution.py:88
  217.0 10.2 %bitcast_add_fusion.4 = f32[1024,3,128]{0,2,1:T(8,128)} fusion(f32[1024,3,128]{0,2,1:T(8,128)} %get-tuple-element.528, f32[3,512,1024]{2,1,0:T(8,128)} %fusion.83, bf16[2,3,512,1024]{3,2,1,0:T(8,128)(2,1)} %get-tuple-element.547, s32[]{:T(128)} %get-tuple-element.527, pred[]{:T(512)S(6)} %compare.3, bf16[1024,3,128]{0,2,1:T(8,128)(2,1)} %get-tuple-element.546, ...), kind=kOutput, calls=%fused_computation.26.clone.1 | convolution fusion | flops 414452224 | bytes 22414340 | tf_op jit(solution)/shard_map/while/body/eval_jaxpr/hqk,qhd->khd/dot_general | solution.py:95
  227.2 9.7 %fusion.84 = f32[2,512,3,128]{3,1,2,0:T(8,128)} fusion(f32[2,512,3,128]{3,1,2,0:T(8,128)} %get-tuple-element.530, s32[]{:T(128)} %get-tuple-element.527, bf16[1024,3,128]{2,0,1:T(8,128)(2,1)} %get-tuple-element.550, f32[3,512,1024]{2,1,0:T(8,128)} %fusion.83, bf16[2,3,512,1024]{3,2,1,0:T(8,128)(2,1)} %get-tuple-element.547), kind=kOutput, calls=%fused_computation.28.clone.1 | convolution fusion | flops 413665792 | bytes 20448768 | tf_op jit(solution)/shard_map/while/body/eval_jaxpr/hqk,khd->qhd/dot_general | solution.py:98
  236.9 3.0 bitcast_add_fusion.5
  241.2 4.9 %fusion.83 = f32[3,512,1024]{2,1,0:T(8,128)} fusion(bf16[1024,3,128]{2,0,1:T(8,128)(2,1)} %get-tuple-element.549, bf16[1024,3,128]{0,2,1:T(8,128)(2,1)} %get-tuple-element.548, s32[]{:T(128)S(6)} %select_n.24), kind=kOutput, calls=%fused_computation.30.clone.1 | convolution fusion | flops 402653184 | bytes 7471108 | tf_op jit(solution)/shard_map/while/body/eval_jaxpr/qhd,khd->hqk/dot_general | solution.py:88
  246.1 10.1 %bitcast_add_fusion.4 = f32[1024,3,128]{0,2,1:T(8,128)} fusion(f32[1024,3,128]{0,2,1:T(8,128)} %get-tuple-element.528, f32[3,512,1024]{2,1,0:T(8,128)} %fusion.83, bf16[2,3,512,1024]{3,2,1,0:T(8,128)(2,1)} %get-tuple-element.547, s32[]{:T(128)} %get-tuple-element.527, pred[]{:T(512)S(6)} %compare.3, bf16[1024,3,128]{0,2,1:T(8,128)(2,1)} %get-tuple-element.546, ...), kind=kOutput, calls=%fused_computation.26.clone.1 | convolution fusion | flops 414452224 | bytes 22414340 | tf_op jit(solution)/shard_map/while/body/eval_jaxpr/hqk,qhd->khd/dot_general | solution.py:95
  256.2 9.3 %fusion.84 = f32[2,512,3,128]{3,1,2,0:T(8,128)} fusion(f32[2,512,3,128]{3,1,2,0:T(8,128)} %get-tuple-element.530, s32[]{:T(128)} %get-tuple-element.527, bf16[1024,3,128]{2,0,1:T(8,128)(2,1)} %get-tuple-element.550, f32[3,512,1024]{2,1,0:T(8,128)} %fusion.83, bf16[2,3,512,1024]{3,2,1,0:T(8,128)(2,1)} %get-tuple-element.547), kind=kOutput, calls=%fused_computation.28.clone.1 | convolution fusion | flops 413665792 | bytes 20448768 | tf_op jit(solution)/shard_map/while/body/eval_jaxpr/hqk,khd->qhd/dot_general | solution.py:98
  265.5 2.9 bitcast_add_fusion.5
  268.5 3.7 copy.156
  272.2 2.7 copy.159
  274.9 3.0 copy.160
  277.9 2.3 multiply_reduce_fusion.3
  280.4 1.6 copy.177
  281.9 3.3 reshape.179
  285.3 4.3 fusion.47
  289.5 6.7 %all-to-all-start.3 = ((bf16[8,128,384]{1,2,0:T(8,128)(2,1)}), bf16[8,128,384]{1,2,0:T(8,128)(2,1)}, u32[]{:S(2)}, u32[]{:S(2)}) async-start(bf16[8,128,384]{1,2,0:T(8,128)(2,1)} %fusion.47), calls=%async_computation.3 | async-start | bytes 1572864 | tf_op jit(solution)/shard_map/all_to_all | solution.py:110
  296.2 2.0 multiply_reduce_fusion
  298.9 1.4 copy.163
  300.3 17.9 %all-to-all-done.3 = bf16[8,128,384]{1,2,0:T(8,128)(2,1)} async-done(((bf16[8,128,384]{1,2,0:T(8,128)(2,1)}), bf16[8,128,384]{1,2,0:T(8,128)(2,1)}, u32[]{:S(2)}, u32[]{:S(2)}) %all-to-all-start.3) | async-done | bytes 786464 | tf_op jit(solution)/shard_map/all_to_all | solution.py:110
  318.2 4.9 %all-to-all-start.4 = ((bf16[8,128,384]{2,1,0:T(8,128)(2,1)}), bf16[8,128,384]{2,1,0:T(8,128)(2,1)S(1)}, u32[]{:S(2)}, u32[]{:S(2)}) async-start(bf16[8,128,384]{2,1,0:T(8,128)(2,1)} %copy.163), calls=%async_computation.4 | async-start | bytes 1572864 | tf_op jit(solution)/shard_map/all_to_all | solution.py:113
  323.4 1.4 copy.165
  324.8 18.6 %all-to-all-done.4 = bf16[8,128,384]{2,1,0:T(8,128)(2,1)S(1)} async-done(((bf16[8,128,384]{2,1,0:T(8,128)(2,1)}), bf16[8,128,384]{2,1,0:T(8,128)(2,1)S(1)}, u32[]{:S(2)}, u32[]{:S(2)}) %all-to-all-start.4) | async-done | bytes 786464 | tf_op jit(solution)/shard_map/all_to_all | solution.py:113
  343.4 5.5 %all-to-all-start.5 = ((bf16[8,128,384]{2,1,0:T(8,128)(2,1)}), bf16[8,128,384]{2,1,0:T(8,128)(2,1)}, u32[]{:S(2)}, u32[]{:S(2)}) async-start(bf16[8,128,384]{2,1,0:T(8,128)(2,1)} %copy.165), calls=%async_computation.5 | async-start | bytes 1572864 | tf_op jit(solution)/shard_map/all_to_all | solution.py:116
  349.0 1.9 reshape.184
  350.9 2.6 multiply_reduce_fusion.1
  353.6 2.4 copy.170
  356.3 1.2 copy.171
  357.5 11.9 %all-to-all-done.5 = bf16[8,128,384]{2,1,0:T(8,128)(2,1)} async-done(((bf16[8,128,384]{2,1,0:T(8,128)(2,1)}), bf16[8,128,384]{2,1,0:T(8,128)(2,1)}, u32[]{:S(2)}, u32[]{:S(2)}) %all-to-all-start.5) | async-done | bytes 786464 | tf_op jit(solution)/shard_map/all_to_all | solution.py:116
  369.4 1.5 copy.166
  372.1 1.6 fusion.51
  373.6 13.2 %all-reduce.2 = (f32[]{:T(128)}, f32[128]{0:T(128)S(1)}, f32[128]{0:T(128)S(1)}) all-reduce(f32[]{:T(128)} %fusion.51, f32[128]{0:T(128)S(1)} %multiply_reduce_fusion.1, f32[128]{0:T(128)S(1)} %get-tuple-element.303), channel_id=1, replica_groups=mesh['dp_0'=4,'dp_1'=4,'dp_2'=2,'seq'=8] {'dp_0'}, use_global_device_ids=true, to_apply=%region_14.15 | all-reduce | flops 257 | bytes 2056 | tf_op jit(solution)/shard_map/psum | solution.py:16
  386.9 11.0 %all-reduce.1 = (f32[]{:T(128)}, f32[128]{0:T(128)S(1)}, f32[128]{0:T(128)S(1)}) all-reduce(f32[]{:T(128)} %get-tuple-element.347, f32[128]{0:T(128)S(1)} %get-tuple-element.348, f32[128]{0:T(128)S(1)} %get-tuple-element.349), channel_id=1, replica_groups=mesh['dp_0'=4,'dp_1'=4,'dp_2'=2,'seq'=8] {'dp_1'}, use_global_device_ids=true, to_apply=%region_15.16 | all-reduce | flops 257 | bytes 2056 | tf_op jit(solution)/shard_map/psum | solution.py:16
  397.9 3.1 all-reduce.3
  401.0 16.2 %all-reduce = (f32[]{:T(128)}, f32[128]{0:T(128)S(1)}, f32[128]{0:T(128)S(1)}) all-reduce(f32[]{:T(128)} %get-tuple-element.350, f32[128]{0:T(128)S(1)} %get-tuple-element.351, f32[128]{0:T(128)S(1)} %get-tuple-element.352), channel_id=1, replica_groups=mesh['dp_0'=4,'dp_1'=4,'dp_2'=2,'seq'=8] {'seq'}, use_global_device_ids=true, to_apply=%region_17.18 | all-reduce | flops 257 | bytes 2056 | tf_op jit(solution)/shard_map/psum | solution.py:16
  420.8 1.6 convert_multiply_fusion.15
  (97 shorter events, 20.7 us)
Async XLA Ops:
  7.2 1.1 copy-start.12
  7.2 181.7 %all-gather.3.cloned.1.call-start = ((), (), s32[]{:S(2)}) async-start(), calls=%async_computation.8 | async-start | bytes 14155776 | tf_op jit(solution)/shard_map/all_gather | solution.py:75
  8.3 9.7 %copy-start.13 = (bf16[1,128,3072]{2,1,0:T(8,128)(2,1)S(1)}, bf16[1,128,3072]{2,1,0:T(8,128)(2,1)}, u32[]{:S(2)}) copy-start(bf16[1,128,3072]{2,1,0:T(8,128)(2,1)} %param.13) | copy-start | bytes 2359300
  9.5 35.9 %all-to-all-start = ((bf16[128,8,384]{0,2,1:T(8,128)(2,1)}), bf16[128,8,384]{0,2,1:T(8,128)(2,1)S(1)}, u32[]{:S(2)}, u32[]{:S(2)}) async-start(bf16[128,8,384]{0,2,1:T(8,128)(2,1)} %bitcast.4), calls=%async_computation | async-start | bytes 1572864 | tf_op jit(solution)/shard_map/all_to_all | solution.py:44
  18.0 33.2 %copy-start.14 = (bf16[1,128,3072]{2,1,0:T(8,128)(2,1)S(1)}, bf16[1,128,3072]{2,1,0:T(8,128)(2,1)}, u32[]{:S(2)}) copy-start(bf16[1,128,3072]{2,1,0:T(8,128)(2,1)} %param.14) | copy-start | bytes 2359300
  45.4 42.6 %copy-start.7 = (bf16[128,8,384]{0,2,1:T(8,128)(2,1)}, bf16[128,8,384]{0,2,1:T(8,128)(2,1)S(1)}, u32[]{:S(2)}) copy-start(bf16[128,8,384]{0,2,1:T(8,128)(2,1)S(1)} %all-to-all-done) | copy-start | bytes 2359300
  45.4 37.0 %all-to-all-start.1 = ((bf16[128,8,384]{0,2,1:T(8,128)(2,1)}), bf16[128,8,384]{0,2,1:T(8,128)(2,1)S(1)}, u32[]{:S(2)}, u32[]{:S(2)}) async-start(bf16[128,8,384]{0,2,1:T(8,128)(2,1)} %bitcast.8), calls=%async_computation.1 | async-start | bytes 1572864 | tf_op jit(solution)/shard_map/all_to_all | solution.py:45
  51.2 36.5 %copy-start.18 = (f32[128]{0:T(128)S(1)}, f32[128]{0:T(128)}, u32[]{:S(2)}) copy-start(f32[128]{0:T(128)} %param.18) | copy-start | bytes 1540
  51.2 36.5 %copy-start.19 = (s32[1,4]{1,0:T(1,128)S(1)}, s32[1,4]{1,0:T(1,128)}, u32[]{:S(2)}) copy-start(s32[1,4]{1,0:T(1,128)} %param.16) | copy-start | bytes 52
  82.4 5.6 %copy-start.11 = (bf16[128,8,384]{0,2,1:T(8,128)(2,1)}, bf16[128,8,384]{0,2,1:T(8,128)(2,1)S(1)}, u32[]{:S(2)}) copy-start(bf16[128,8,384]{0,2,1:T(8,128)(2,1)S(1)} %all-to-all-done.1) | copy-start | bytes 2359300
  82.4 36.3 %all-to-all-start.2 = ((bf16[128,8,384]{0,2,1:T(8,128)(2,1)}), bf16[128,8,384]{0,2,1:T(8,128)(2,1)}, u32[]{:S(2)}, u32[]{:S(2)}) async-start(bf16[128,8,384]{0,2,1:T(8,128)(2,1)} %bitcast.10), calls=%async_computation.2 | async-start | bytes 1572864 | tf_op jit(solution)/shard_map/all_to_all | solution.py:46
  87.7 284.4 %reduce-scatter.2.cloned.1.call-start = ((), (), s32[]{:S(2)}) async-start(), calls=%async_computation.7 | async-start | bytes 4866048 | tf_op jit(solution)/shard_map/reduce_scatter | solution.py:120
  89.0 1.7 copy-start.4
  95.6 0.7 copy-start.17
  125.7 1.9 copy-start.3
  130.5 3.5 copy-start
  134.0 1.9 copy-start.2
  134.0 1.9 copy-start.15
  135.9 2.6 copy-start.1
  138.5 0.9 copy-start.16
  141.1 3.5 copy-start
  144.5 1.9 copy-start.2
  144.5 1.9 copy-start.15
  146.5 2.6 copy-start.1
  149.1 0.9 copy-start.16
  289.5 28.7 %all-to-all-start.3 = ((bf16[8,128,384]{1,2,0:T(8,128)(2,1)}), bf16[8,128,384]{1,2,0:T(8,128)(2,1)}, u32[]{:S(2)}, u32[]{:S(2)}) async-start(bf16[8,128,384]{1,2,0:T(8,128)(2,1)} %fusion.47), calls=%async_computation.3 | async-start | bytes 1572864 | tf_op jit(solution)/shard_map/all_to_all | solution.py:110
  296.2 2.0 copy-start.8
  318.2 25.2 %all-to-all-start.4 = ((bf16[8,128,384]{2,1,0:T(8,128)(2,1)}), bf16[8,128,384]{2,1,0:T(8,128)(2,1)S(1)}, u32[]{:S(2)}, u32[]{:S(2)}) async-start(bf16[8,128,384]{2,1,0:T(8,128)(2,1)} %copy.163), calls=%async_computation.4 | async-start | bytes 1572864 | tf_op jit(solution)/shard_map/all_to_all | solution.py:113
  323.4 25.6 %copy-start.5 = (f32[8,128,384]{1,0,2:T(8,128)S(1)}, f32[8,128,384]{1,0,2:T(8,128)}, u32[]{:S(2)}) copy-start(f32[8,128,384]{1,0,2:T(8,128)} %copy-done.4) | copy-start | bytes 4718596
  343.4 5.5 %copy-start.9 = (bf16[8,128,384]{2,1,0:T(8,128)(2,1)}, bf16[8,128,384]{2,1,0:T(8,128)(2,1)S(1)}, u32[]{:S(2)}) copy-start(bf16[8,128,384]{2,1,0:T(8,128)(2,1)S(1)} %all-to-all-done.4) | copy-start | bytes 2359300
  343.4 25.9 %all-to-all-start.5 = ((bf16[8,128,384]{2,1,0:T(8,128)(2,1)}), bf16[8,128,384]{2,1,0:T(8,128)(2,1)}, u32[]{:S(2)}, u32[]{:S(2)}) async-start(bf16[8,128,384]{2,1,0:T(8,128)(2,1)} %copy.165), calls=%async_computation.5 | async-start | bytes 1572864 | tf_op jit(solution)/shard_map/all_to_all | solution.py:116
  349.0 1.9 copy-start.6
  353.6 2.4 copy-start.10
Sparse Core Ops, SparseCore 0:
  9.8 179.0 all-gather.2
  200.5 91.9 reduce-scatter.1
where the time goes:
time: 432 us; the launch traced here: 430 us
  waiting for transfers between devices  156 us (36%)
  matrix products  86.1 us (20%)
  local copies, waits for them, and re-layouts  60.2 us (14%)
  blocking collectives  43.5 us (10%)
  starting transfers between devices  36.9 us (9%)
  other arithmetic  26.9 us (6%)
  between operations  17.5 us (4%)
    psum x4, blocking collectives, one_axis_at_a_time(): array = lax.psum(array, axis)  43.5 us
    all_gather x1, waiting for transfers between devices, local(): out_full = lax.all_gather(out_grad[0], 'seq', axis=0, tiled=True)  32.1 us
    all_to_all x1, waiting for transfers between devices, local(): lax.all_to_all(key_rows[0], 'seq', split_axis=1, concat_axis=0, tiled=True)  30 us
    all_to_all x1, waiting for transfers between devices, local(): lax.all_to_all(query_rows[0], 'seq', split_axis=1, concat_axis=0, tiled=T...  26.2 us
    dot_general x2, matrix products, backward_block(): jnp.einsum('hqk,qhd->khd', d_scores, query_block, preferred_element_type=...  20.3 us
    all_to_all x1, waiting for transfers between devices, local(): lax.all_to_all(value_rows[0], 'seq', split_axis=1, concat_axis=0, tiled=T...  19.1 us
    dot_general x2, matrix products, backward_block(): jnp.einsum('hqk,khd->qhd', d_scores, k_norm, preferred_element_type=jnp.f...  19 us
    all_to_all x1, waiting for transfers between devices, local(): lax.all_to_all(key_grad.reshape(total, width), 'seq', split_axis=0, conca...  18.6 us
  transfers between devices with their start and end apart: 8, of which 7 were waited for; matrix products, arithmetic and copies ran while one was open for 35% of the time, Pallas kernels for 0%

commit v1 on v0

--- a/solution.py
+++ b/solution.py
@@ -13,7 +13,8 @@
 
 def one_axis_at_a_time(array, axes):
     for axis in axes:
-        array = lax.psum(array, axis)
+        upper = lax.all_gather(array, axis_name=axis)
+        array = jnp.sum(upper, axis=0)
     return array
 
 

time: 432 us -> 491 us (1.14)
  blocking collectives: 43.5 us -> 104 us
  waiting for transfers between devices: 156 us -> 145 us
  local copies, waits for them, and re-layouts: 60.2 us -> 68.2 us
    all_gather x0 -> x8, blocking collectives: none -> 67.2 us  [one_axis_at_a_time(): upper = lax.all_gather(array, axis_name=axis)]
    psum x4 -> x0, blocking collectives: 43.5 us -> none  [one_axis_at_a_time(): array = lax.psum(array, axis)]
    unnamed x0 -> x4, blocking collectives: none -> 37.2 us
    all_to_all x1, waiting for transfers between devices: 11.9 us -> 0.01 us  [local(): lax.all_to_all(value_grad.reshape(total, width), 'seq', split_axis=0, con...]
    unnamed x41 -> x63, local copies, waits for them, and re-layouts: 14.8 us -> 22.7 us
  transfers between devices with their start and end apart: 8 -> 8, of which waited for: 7 -> 6; matrix products, arithmetic and copies ran while one was open for 35% -> 33% of each run, Pallas kernels for 0% -> 0%
where the time goes in v1:
time: 491 us; the launch traced here: 489 us
  waiting for transfers between devices  145 us (30%)
  blocking collectives  104 us (21%)
  matrix products  86.1 us (18%)
  local copies, waits for them, and re-layouts  68.2 us (14%)
  starting transfers between devices  36.9 us (8%)
  other arithmetic  28.8 us (6%)
  between operations  17.5 us (4%)
    all_gather x8, blocking collectives, one_axis_at_a_time(): upper = lax.all_gather(array, axis_name=axis)  67.2 us
    unnamed x4, blocking collectives  37.2 us
    all_gather x1, waiting for transfers between devices, local(): out_full = lax.all_gather(out_grad[0], 'seq', axis=0, tiled=True)  32.1 us
    all_to_all x1, waiting for transfers between devices, local(): lax.all_to_all(key_rows[0], 'seq', split_axis=1, concat_axis=0, tiled=True)  30 us
    all_to_all x1, waiting for transfers between devices, local(): lax.all_to_all(query_rows[0], 'seq', split_axis=1, concat_axis=0, tiled=T...  26.2 us
    unnamed x63, local copies, waits for them, and re-layouts  22.7 us
    dot_general x2, matrix products, backward_block(): jnp.einsum('hqk,qhd->khd', d_scores, query_block, preferred_element_type=...  20.3 us
    all_to_all x1, waiting for transfers between devices, local(): lax.all_to_all(value_rows[0], 'seq', split_axis=1, concat_axis=0, tiled=T...  19.1 us
  transfers between devices with their start and end apart: 8, of which 6 were waited for; matrix products, arithmetic and copies ran while one was open for 33% of the time, Pallas kernels for 0%

profile of v1, /device:TPU:32, one launch (start us, length us, event | category | flops | bytes accessed | tf_op | source)
XLA Modules:
  0.0 489.1 jit_solution(17965438755989849213)
XLA Ops:
  9.5 8.6 %all-to-all-start = ((bf16[128,8,384]{0,2,1:T(8,128)(2,1)}), bf16[128,8,384]{0,2,1:T(8,128)(2,1)S(1)}, u32[]{:S(2)}, u32[]{:S(2)}) async-start(bf16[128,8,384]{0,2,1:T(8,128)(2,1)} %bitcast.4), calls=%async_computation | async-start | bytes 1572864 | tf_op jit(solution)/shard_map/all_to_all | solution.py:45
  19.2 26.2 %all-to-all-done = bf16[128,8,384]{0,2,1:T(8,128)(2,1)S(1)} async-done(((bf16[128,8,384]{0,2,1:T(8,128)(2,1)}), bf16[128,8,384]{0,2,1:T(8,128)(2,1)S(1)}, u32[]{:S(2)}, u32[]{:S(2)}) %all-to-all-start) | async-done | bytes 786464 | tf_op jit(solution)/shard_map/all_to_all | solution.py:45
  45.4 5.8 %all-to-all-start.1 = ((bf16[128,8,384]{0,2,1:T(8,128)(2,1)}), bf16[128,8,384]{0,2,1:T(8,128)(2,1)S(1)}, u32[]{:S(2)}, u32[]{:S(2)}) async-start(bf16[128,8,384]{0,2,1:T(8,128)(2,1)} %bitcast.8), calls=%async_computation.1 | async-start | bytes 1572864 | tf_op jit(solution)/shard_map/all_to_all | solution.py:46
  52.3 30.0 %all-to-all-done.1 = bf16[128,8,384]{0,2,1:T(8,128)(2,1)S(1)} async-done(((bf16[128,8,384]{0,2,1:T(8,128)(2,1)}), bf16[128,8,384]{0,2,1:T(8,128)(2,1)S(1)}, u32[]{:S(2)}, u32[]{:S(2)}) %all-to-all-start.1) | async-done | bytes 786464 | tf_op jit(solution)/shard_map/all_to_all | solution.py:46
  82.4 5.3 %all-to-all-start.2 = ((bf16[128,8,384]{0,2,1:T(8,128)(2,1)}), bf16[128,8,384]{0,2,1:T(8,128)(2,1)}, u32[]{:S(2)}, u32[]{:S(2)}) async-start(bf16[128,8,384]{0,2,1:T(8,128)(2,1)} %bitcast.10), calls=%async_computation.2 | async-start | bytes 1572864 | tf_op jit(solution)/shard_map/all_to_all | solution.py:47
  89.1 1.6 reshape.182
  92.0 2.1 copy.147
  94.1 1.5 reshape.183
  97.4 2.3 copy.151
  99.7 19.1 %all-to-all-done.2 = bf16[128,8,384]{0,2,1:T(8,128)(2,1)} async-done(((bf16[128,8,384]{0,2,1:T(8,128)(2,1)}), bf16[128,8,384]{0,2,1:T(8,128)(2,1)}, u32[]{:S(2)}, u32[]{:S(2)}) %all-to-all-start.2) | async-done | bytes 786464 | tf_op jit(solution)/shard_map/all_to_all | solution.py:47
  118.7 2.5 copy.149
  121.2 2.2 reshape.177
  123.4 2.3 copy.152
  125.7 1.7 multiply_reduce_fusion.5
  128.8 21.1 %while.27 = (s32[]{:T(128)}, bf16[2,3,512,1024]{3,2,1,0:T(8,128)(2,1)}, bf16[2,512,3,128]{3,1,2,0:T(8,128)(2,1)}, s32[2]{0:T(128)S(1)}, s32[1024]{0:T(1024)S(1)}...) while((s32[]{:T(128)}, ...), condition=%wide.region_6.7_spmd, body=%wide.region_4.6_spmd.sunk | while | flops 817035776 | bytes 85746000 | solution.py:74
  130.5 3.4 fusion.75
  134.0 1.9 bitcast_dynamic-update-slice_fusion.2
  137.0 1.5 copy-done.1
  141.1 3.4 fusion.75
  144.5 1.9 bitcast_dynamic-update-slice_fusion.2
  149.9 3.1 copy.167
  153.0 2.1 copy.180
  156.8 32.1 %all-gather.19.cloned.1.call-done = bf16[1,1024,6144]{2,1,0:T(8,128)(2,1)} async-done(((bf16[1,128,6144]{2,1,0:T(8,128)(2,1)}), bf16[1,1024,6144]{2,1,0:T(8,128)(2,1)}) %all-gather.19.cloned.1.call-update) | async-done | bytes 12582928 | tf_op jit(solution)/shard_map/all_gather | solution.py:76
  188.9 11.4 %fusion.42 = bf16[384,6144]{0,1:T(8,128)(2,1)} fusion(bf16[1024,384]{0,1:T(8,128)(2,1)} %bitcast.177, bf16[1,1024,6144]{2,1,0:T(8,128)(2,1)} %all-gather.19.cloned.1.call-done), kind=kOutput, calls=%fused_computation.45 | convolution fusion | flops 4834197504 | bytes 18087936 | tf_op jit(solution)/shard_map/dot_general | solution.py:77
  200.3 10.4 %fusion.48 = bf16[1024,384]{0,1:T(8,128)(2,1)} fusion(bf16[384,6144]{1,0:T(8,128)(2,1)} %param.17, bf16[1,1024,6144]{2,1,0:T(8,128)(2,1)} %all-gather.19.cloned.1.call-done), kind=kOutput, calls=%fused_computation.62 | convolution fusion | flops 4832231424 | bytes 18087936 | tf_op jit(solution)/shard_map/dot_general | solution.py:78
  210.8 57.7 %while.28 = (s32[]{:T(128)}, f32[1024,3,128]{0,2,1:T(8,128)}, f32[1024,3,128]{0,2,1:T(8,128)S(1)}, f32[2,512,3,128]{3,1,2,0:T(8,128)}, s32[2]{0:T(128)S(1)}, /*i...) while((s32[]{:T(128)}, f32[1024,3,128]{0,2,1:T(8,128)}, ...), condition=%wide.region_9.10_spmd.clone, body=%wide.region_7.9_spmd.clone.sunk | while | flops 1634210816 | bytes 57019604 | solution.py:103
  212.0 5.0 %fusion.83 = f32[3,512,1024]{2,1,0:T(8,128)} fusion(bf16[1024,3,128]{2,0,1:T(8,128)(2,1)} %get-tuple-element.537, bf16[1024,3,128]{0,2,1:T(8,128)(2,1)} %get-tuple-element.536, s32[]{:T(128)S(6)} %select_n.24), kind=kOutput, calls=%fused_computation.30.clone.1 | convolution fusion | flops 402653184 | bytes 7471108 | tf_op jit(solution)/shard_map/while/body/eval_jaxpr/qhd,khd->hqk/dot_general | solution.py:89
  217.0 10.2 %bitcast_add_fusion.4 = f32[1024,3,128]{0,2,1:T(8,128)} fusion(f32[1024,3,128]{0,2,1:T(8,128)} %get-tuple-element.516, f32[3,512,1024]{2,1,0:T(8,128)} %fusion.83, bf16[2,3,512,1024]{3,2,1,0:T(8,128)(2,1)} %get-tuple-element.535, s32[]{:T(128)} %get-tuple-element.515, pred[]{:T(512)S(6)} %compare.3, bf16[1024,3,128]{0,2,1:T(8,128)(2,1)} %get-tuple-element.534, ...), kind=kOutput, calls=%fused_computation.26.clone.1 | convolution fusion | flops 414452224 | bytes 22414340 | tf_op jit(solution)/shard_map/while/body/eval_jaxpr/hqk,qhd->khd/dot_general | solution.py:96
  227.2 9.7 %fusion.84 = f32[2,512,3,128]{3,1,2,0:T(8,128)} fusion(f32[2,512,3,128]{3,1,2,0:T(8,128)} %get-tuple-element.518, s32[]{:T(128)} %get-tuple-element.515, bf16[1024,3,128]{2,0,1:T(8,128)(2,1)} %get-tuple-element.538, f32[3,512,1024]{2,1,0:T(8,128)} %fusion.83, bf16[2,3,512,1024]{3,2,1,0:T(8,128)(2,1)} %get-tuple-element.535), kind=kOutput, calls=%fused_computation.28.clone.1 | convolution fusion | flops 413665792 | bytes 20448768 | tf_op jit(solution)/shard_map/while/body/eval_jaxpr/hqk,khd->qhd/dot_general | solution.py:99
  236.9 3.0 bitcast_add_fusion.5
  241.2 4.9 %fusion.83 = f32[3,512,1024]{2,1,0:T(8,128)} fusion(bf16[1024,3,128]{2,0,1:T(8,128)(2,1)} %get-tuple-element.537, bf16[1024,3,128]{0,2,1:T(8,128)(2,1)} %get-tuple-element.536, s32[]{:T(128)S(6)} %select_n.24), kind=kOutput, calls=%fused_computation.30.clone.1 | convolution fusion | flops 402653184 | bytes 7471108 | tf_op jit(solution)/shard_map/while/body/eval_jaxpr/qhd,khd->hqk/dot_general | solution.py:89
  246.1 10.1 %bitcast_add_fusion.4 = f32[1024,3,128]{0,2,1:T(8,128)} fusion(f32[1024,3,128]{0,2,1:T(8,128)} %get-tuple-element.516, f32[3,512,1024]{2,1,0:T(8,128)} %fusion.83, bf16[2,3,512,1024]{3,2,1,0:T(8,128)(2,1)} %get-tuple-element.535, s32[]{:T(128)} %get-tuple-element.515, pred[]{:T(512)S(6)} %compare.3, bf16[1024,3,128]{0,2,1:T(8,128)(2,1)} %get-tuple-element.534, ...), kind=kOutput, calls=%fused_computation.26.clone.1 | convolution fusion | flops 414452224 | bytes 22414340 | tf_op jit(solution)/shard_map/while/body/eval_jaxpr/hqk,qhd->khd/dot_general | solution.py:96
  256.2 9.3 %fusion.84 = f32[2,512,3,128]{3,1,2,0:T(8,128)} fusion(f32[2,512,3,128]{3,1,2,0:T(8,128)} %get-tuple-element.518, s32[]{:T(128)} %get-tuple-element.515, bf16[1024,3,128]{2,0,1:T(8,128)(2,1)} %get-tuple-element.538, f32[3,512,1024]{2,1,0:T(8,128)} %fusion.83, bf16[2,3,512,1024]{3,2,1,0:T(8,128)(2,1)} %get-tuple-element.535), kind=kOutput, calls=%fused_computation.28.clone.1 | convolution fusion | flops 413665792 | bytes 20448768 | tf_op jit(solution)/shard_map/while/body/eval_jaxpr/hqk,khd->qhd/dot_general | solution.py:99
  265.5 2.9 bitcast_add_fusion.5
  268.5 3.7 copy.156
  272.2 2.7 copy.159
  274.9 3.0 copy.160
  277.9 2.3 multiply_reduce_fusion.3
  280.4 1.6 copy.177
  281.9 3.3 reshape.179
  285.3 4.3 fusion.47
  289.5 6.7 %all-to-all-start.3 = ((bf16[8,128,384]{1,2,0:T(8,128)(2,1)}), bf16[8,128,384]{1,2,0:T(8,128)(2,1)}, u32[]{:S(2)}, u32[]{:S(2)}) async-start(bf16[8,128,384]{1,2,0:T(8,128)(2,1)} %fusion.47), calls=%async_computation.3 | async-start | bytes 1572864 | tf_op jit(solution)/shard_map/all_to_all | solution.py:111
  296.2 2.0 multiply_reduce_fusion
  300.3 17.9 %all-to-all-done.3 = bf16[8,128,384]{1,2,0:T(8,128)(2,1)} async-done(((bf16[8,128,384]{1,2,0:T(8,128)(2,1)}), bf16[8,128,384]{1,2,0:T(8,128)(2,1)}, u32[]{:S(2)}, u32[]{:S(2)}) %all-to-all-start.3) | async-done | bytes 786464 | tf_op jit(solution)/shard_map/all_to_all | solution.py:111
  318.2 4.9 %all-to-all-start.4 = ((bf16[8,128,384]{2,1,0:T(8,128)(2,1)}), bf16[8,128,384]{2,1,0:T(8,128)(2,1)S(1)}, u32[]{:S(2)}, u32[]{:S(2)}) async-start(bf16[8,128,384]{2,1,0:T(8,128)(2,1)} %copy.163), calls=%async_computation.4 | async-start | bytes 1572864 | tf_op jit(solution)/shard_map/all_to_all | solution.py:114
  324.8 18.6 %all-to-all-done.4 = bf16[8,128,384]{2,1,0:T(8,128)(2,1)S(1)} async-done(((bf16[8,128,384]{2,1,0:T(8,128)(2,1)}), bf16[8,128,384]{2,1,0:T(8,128)(2,1)S(1)}, u32[]{:S(2)}, u32[]{:S(2)}) %all-to-all-start.4) | async-done | bytes 786464 | tf_op jit(solution)/shard_map/all_to_all | solution.py:114
  343.4 5.5 %all-to-all-start.5 = ((bf16[8,128,384]{2,1,0:T(8,128)(2,1)}), bf16[8,128,384]{2,1,0:T(8,128)(2,1)}, u32[]{:S(2)}, u32[]{:S(2)}) async-start(bf16[8,128,384]{2,1,0:T(8,128)(2,1)} %copy.165), calls=%async_computation.5 | async-start | bytes 1572864 | tf_op jit(solution)/shard_map/all_to_all | solution.py:117
  351.4 1.9 reshape.184
  353.3 2.6 multiply_reduce_fusion.1
  356.0 10.1 %all-gather.9 = f32[4,1,128]{2,1,0:T(1,128)S(1)} all-gather(f32[1,1,128]{2,1,0:T(1,128)S(1)} %bitcast.183), channel_id=3, replica_groups=mesh['dp_0'=4,'dp_1'=4,'dp_2'=2,'seq'=8] {'dp_0'}, dimensions={0}, use_global_device_ids=true | all-gather | bytes 2560 | tf_op jit(solution)/shard_map/all_gather | solution.py:16
  366.1 9.7 %all-gather.10 = f32[4,1,128]{2,1,0:T(1,128)S(1)} all-gather(f32[1,1,128]{2,1,0:T(1,128)S(1)} %bitcast.179), channel_id=4, replica_groups=mesh['dp_0'=4,'dp_1'=4,'dp_2'=2,'seq'=8] {'dp_1'}, dimensions={0}, use_global_device_ids=true | all-gather | bytes 2560 | tf_op jit(solution)/shard_map/all_gather | solution.py:16
  375.8 1.8 all-gather.11
  377.6 14.8 %all-gather.12 = f32[8,1,128]{2,1,0:T(1,128)S(1)} all-gather(f32[1,1,128]{2,1,0:T(1,128)S(1)} %bitcast.180), channel_id=6, replica_groups=mesh['dp_0'=4,'dp_1'=4,'dp_2'=2,'seq'=8] {'seq'}, dimensions={0}, use_global_device_ids=true | all-gather | bytes 4608 | tf_op jit(solution)/shard_map/all_gather | solution.py:16
  392.4 7.0 %all-gather.13 = f32[4,1,128]{2,1,0:T(1,128)S(1)} all-gather(f32[1,1,128]{2,1,0:T(1,128)S(1)} %bitcast.178), channel_id=7, replica_groups=mesh['dp_0'=4,'dp_1'=4,'dp_2'=2,'seq'=8] {'dp_0'}, dimensions={0}, use_global_device_ids=true | all-gather | bytes 2560 | tf_op jit(solution)/shard_map/all_gather | solution.py:16
  399.4 7.0 %all-gather.14 = f32[4,1,128]{2,1,0:T(1,128)S(1)} all-gather(f32[1,1,128]{2,1,0:T(1,128)S(1)} %bitcast.181), channel_id=8, replica_groups=mesh['dp_0'=4,'dp_1'=4,'dp_2'=2,'seq'=8] {'dp_1'}, dimensions={0}, use_global_device_ids=true | all-gather | bytes 2560 | tf_op jit(solution)/shard_map/all_gather | solution.py:16
  406.4 1.8 all-gather.15
  408.2 15.1 %all-gather.16 = f32[8,1,128]{2,1,0:T(1,128)S(1)} all-gather(f32[1,1,128]{2,1,0:T(1,128)S(1)} %bitcast.182), channel_id=10, replica_groups=mesh['dp_0'=4,'dp_1'=4,'dp_2'=2,'seq'=8] {'seq'}, dimensions={0}, use_global_device_ids=true | all-gather | bytes 4608 | tf_op jit(solution)/shard_map/all_gather | solution.py:16
  424.6 2.3 copy.170
  426.9 1.6 fusion.51
  430.3 9.8 %all-reduce = f32[4]{0:T(128)S(1)} all-reduce(f32[4]{0:T(128)S(1)} %dynamic-update-slice), channel_id=1, replica_groups=mesh['dp_0'=4,'dp_1'=4,'dp_2'=2,'seq'=8] {'dp_0'}, use_global_device_ids=true, to_apply=%add | all-reduce | flops 4 | bytes 32
  443.2 9.7 %all-reduce.1 = f32[4]{0:T(128)S(1)} all-reduce(f32[4]{0:T(128)S(1)} %dynamic-update-slice.1), channel_id=1, replica_groups=mesh['dp_0'=4,'dp_1'=4,'dp_2'=2,'seq'=8] {'dp_1'}, use_global_device_ids=true, to_apply=%add.1 | all-reduce | flops 4 | bytes 32
  454.9 1.5 copy.166
  456.5 2.5 all-reduce.2
  462.1 15.3 %all-reduce.3 = f32[8]{0:T(128)S(1)} all-reduce(f32[8]{0:T(128)S(1)} %dynamic-update-slice.3), channel_id=1, replica_groups=mesh['dp_0'=4,'dp_1'=4,'dp_2'=2,'seq'=8] {'seq'}, use_global_device_ids=true, to_apply=%add.3 | all-reduce | flops 8 | bytes 64
  (139 shorter events, 40.3 us)
Async XLA Ops:
  7.2 1.1 copy-start.12
  7.2 181.7 %all-gather.19.cloned.1.call-start = ((), (), s32[]{:S(2)}) async-start(), calls=%async_computation.8 | async-start | bytes 14155776 | tf_op jit(solution)/shard_map/all_gather | solution.py:76
  8.3 9.7 %copy-start.13 = (bf16[1,128,3072]{2,1,0:T(8,128)(2,1)S(1)}, bf16[1,128,3072]{2,1,0:T(8,128)(2,1)}, u32[]{:S(2)}) copy-start(bf16[1,128,3072]{2,1,0:T(8,128)(2,1)} %param.13) | copy-start | bytes 2359300
  9.5 35.9 %all-to-all-start = ((bf16[128,8,384]{0,2,1:T(8,128)(2,1)}), bf16[128,8,384]{0,2,1:T(8,128)(2,1)S(1)}, u32[]{:S(2)}, u32[]{:S(2)}) async-start(bf16[128,8,384]{0,2,1:T(8,128)(2,1)} %bitcast.4), calls=%async_computation | async-start | bytes 1572864 | tf_op jit(solution)/shard_map/all_to_all | solution.py:45
  18.0 33.2 %copy-start.14 = (bf16[1,128,3072]{2,1,0:T(8,128)(2,1)S(1)}, bf16[1,128,3072]{2,1,0:T(8,128)(2,1)}, u32[]{:S(2)}) copy-start(bf16[1,128,3072]{2,1,0:T(8,128)(2,1)} %param.14) | copy-start | bytes 2359300
  45.4 42.7 %copy-start.7 = (bf16[128,8,384]{0,2,1:T(8,128)(2,1)}, bf16[128,8,384]{0,2,1:T(8,128)(2,1)S(1)}, u32[]{:S(2)}) copy-start(bf16[128,8,384]{0,2,1:T(8,128)(2,1)S(1)} %all-to-all-done) | copy-start | bytes 2359300
  45.4 37.0 %all-to-all-start.1 = ((bf16[128,8,384]{0,2,1:T(8,128)(2,1)}), bf16[128,8,384]{0,2,1:T(8,128)(2,1)S(1)}, u32[]{:S(2)}, u32[]{:S(2)}) async-start(bf16[128,8,384]{0,2,1:T(8,128)(2,1)} %bitcast.8), calls=%async_computation.1 | async-start | bytes 1572864 | tf_op jit(solution)/shard_map/all_to_all | solution.py:46
  51.2 36.5 %copy-start.19 = (f32[128]{0:T(128)S(1)}, f32[128]{0:T(128)}, u32[]{:S(2)}) copy-start(f32[128]{0:T(128)} %param.18) | copy-start | bytes 1540
  51.2 36.5 %copy-start.20 = (s32[1,4]{1,0:T(1,128)S(1)}, s32[1,4]{1,0:T(1,128)}, u32[]{:S(2)}) copy-start(s32[1,4]{1,0:T(1,128)} %param.16) | copy-start | bytes 52
  82.4 5.3 %copy-start.11 = (bf16[128,8,384]{0,2,1:T(8,128)(2,1)}, bf16[128,8,384]{0,2,1:T(8,128)(2,1)S(1)}, u32[]{:S(2)}) copy-start(bf16[128,8,384]{0,2,1:T(8,128)(2,1)S(1)} %all-to-all-done.1) | copy-start | bytes 2359300
  82.4 36.3 %all-to-all-start.2 = ((bf16[128,8,384]{0,2,1:T(8,128)(2,1)}), bf16[128,8,384]{0,2,1:T(8,128)(2,1)}, u32[]{:S(2)}, u32[]{:S(2)}) async-start(bf16[128,8,384]{0,2,1:T(8,128)(2,1)} %bitcast.10), calls=%async_computation.2 | async-start | bytes 1572864 | tf_op jit(solution)/shard_map/all_to_all | solution.py:47
  87.7 339.2 %reduce-scatter.2.cloned.1.call-start = ((), (), s32[]{:S(2)}) async-start(), calls=%async_computation.7 | async-start | bytes 4866048 | tf_op jit(solution)/shard_map/reduce_scatter | solution.py:121
  89.0 1.7 copy-start.4
  95.6 0.7 copy-start.18
  125.7 1.9 copy-start.3
  130.5 3.5 copy-start
  134.0 1.9 copy-start.2
  134.0 1.9 copy-start.15
  135.9 2.6 copy-start.1
  138.5 0.9 copy-start.16
  141.1 3.5 copy-start
  144.5 1.9 copy-start.2
  144.5 1.9 copy-start.15
  146.5 2.6 copy-start.1
  149.1 0.9 copy-start.16
  289.5 28.7 %all-to-all-start.3 = ((bf16[8,128,384]{1,2,0:T(8,128)(2,1)}), bf16[8,128,384]{1,2,0:T(8,128)(2,1)}, u32[]{:S(2)}, u32[]{:S(2)}) async-start(bf16[8,128,384]{1,2,0:T(8,128)(2,1)} %fusion.47), calls=%async_computation.3 | async-start | bytes 1572864 | tf_op jit(solution)/shard_map/all_to_all | solution.py:111
  296.2 2.0 copy-start.8
  318.2 25.2 %all-to-all-start.4 = ((bf16[8,128,384]{2,1,0:T(8,128)(2,1)}), bf16[8,128,384]{2,1,0:T(8,128)(2,1)S(1)}, u32[]{:S(2)}, u32[]{:S(2)}) async-start(bf16[8,128,384]{2,1,0:T(8,128)(2,1)} %copy.163), calls=%async_computation.4 | async-start | bytes 1572864 | tf_op jit(solution)/shard_map/all_to_all | solution.py:114
  323.4 25.6 %copy-start.24 = (u32[256]{0:T(256)S(1)}, u32[256]{0:T(256)}, u32[]{:S(2)}) copy-start(u32[256]{0:T(256)} %constant.70) | copy-start | bytes 3076
  323.4 26.1 %copy-start.23 = (u32[256]{0:T(256)S(1)}, u32[256]{0:T(256)}, u32[]{:S(2)}) copy-start(u32[256]{0:T(256)} %constant.75) | copy-start | bytes 3076
  323.4 26.7 %copy-start.22 = (u32[256]{0:T(256)S(1)}, u32[256]{0:T(256)}, u32[]{:S(2)}) copy-start(u32[256]{0:T(256)} %constant.80) | copy-start | bytes 3076
  323.5 27.3 %copy-start.21 = (u32[256]{0:T(256)S(1)}, u32[256]{0:T(256)}, u32[]{:S(2)}) copy-start(u32[256]{0:T(256)} %constant.85) | copy-start | bytes 3076
  323.5 27.9 %copy-start.5 = (f32[8,128,384]{1,0,2:T(8,128)S(1)}, f32[8,128,384]{1,0,2:T(8,128)}, u32[]{:S(2)}) copy-start(f32[8,128,384]{1,0,2:T(8,128)} %copy-done.4) | copy-start | bytes 4718596
  343.4 7.9 %copy-start.9 = (bf16[8,128,384]{2,1,0:T(8,128)(2,1)}, bf16[8,128,384]{2,1,0:T(8,128)(2,1)S(1)}, u32[]{:S(2)}) copy-start(bf16[8,128,384]{2,1,0:T(8,128)(2,1)S(1)} %all-to-all-done.4) | copy-start | bytes 2359300
  343.4 111.5 %all-to-all-start.5 = ((bf16[8,128,384]{2,1,0:T(8,128)(2,1)}), bf16[8,128,384]{2,1,0:T(8,128)(2,1)}, u32[]{:S(2)}, u32[]{:S(2)}) async-start(bf16[8,128,384]{2,1,0:T(8,128)(2,1)} %copy.165), calls=%async_computation.5 | async-start | bytes 1572864 | tf_op jit(solution)/shard_map/all_to_all | solution.py:117
  351.4 1.9 copy-start.6
  356.0 73.9 %copy-start.10 = (bf16[8,128,384]{2,1,0:T(8,128)(2,1)S(1)}, bf16[8,128,384]{2,1,0:T(8,128)(2,1)}, u32[]{:S(2)}) copy-start(bf16[8,128,384]{2,1,0:T(8,128)(2,1)} %copy-done.9) | copy-start | bytes 2359300
  454.9 25.5 %copy-start.17 = (bf16[384,192]{0,1:T(8,128)(2,1)S(1)}, bf16[384,192]{0,1:T(8,128)(2,1)}, u32[]{:S(2)}) copy-start(bf16[384,192]{0,1:T(8,128)(2,1)} %reduce-scatter.2.cloned.1.call-done) | copy-start | bytes 442372
Sparse Core Ops, SparseCore 0:
  9.8 179.0 all-gather.18
  200.5 91.9 reduce-scatter.1
